TPU v7x, 32 devices: a whole 2x2x4 slice. The times are simulated.
32 devices in a mesh: dp: 8 (over z, y), head: 4 (over x, core).
Axes of the slice: x: 2, y: 2, z: 4, core: 2. Of those that a mesh axis runs over, the one named last changes fastest.
Arguments:
- q_latent: bfloat16 [1024, 1536], P('dp'), may hold values from -1000 to 1000
- kv_latent: bfloat16 [1024, 576], P('dp'), may hold values from -6 to 6
- kv_gain: float32 [512], replicated, may hold values from 0.1 to 1.9
- w_q_b: bfloat16 [1536, 12288], P(None, 'head'), may hold values from -0.15625 to 0.15625
- w_kv_b: bfloat16 [512, 16384], P(None, 'head'), may hold values from -0.25 to 0.25
- w_o: bfloat16 [8192, 7168], P('head', 'dp'), may hold values from -0.375 to 0.375
- prompt_len: int32 [1], replicated, may hold values from 1 to 255
- response_mask: int32 [1024], replicated, may hold values 0 or 1
Outputs:
- mixed: bfloat16 [1024, 7168], P('dp', 'head')
All inputs are finite; a program needn't handle non-finite values.
Results may differ from a plain program's by a relative error of at most 0.013.
The roundings to bfloat16 on the way count: a program that leaves them out, or rounds other values in their place, can miss the bound.
Values may be sent and summed in bfloat16 or wider, within the bound.
A program may use at most 192 MiB of HBM per device.

v0:
```python
import math

import jax
import jax.numpy as jnp
from jax import lax
from jax.sharding import PartitionSpec as P

KVR = 512
ROPE = 64
NOPE = 128
VD = 128


epsilon = 1e-06


def tables(positions):
    half_width = ROPE // 2
    frequency = 10000.0 ** (-jnp.arange(half_width, dtype=jnp.float32) * 2.0 / ROPE)
    angles = positions.astype(jnp.float32)[:, None] * frequency[None, :]
    return (jnp.cos(angles), jnp.sin(angles))


def rotate(values, cosine, sine_table):
    half_width = values.shape[-1] // 2
    leading = values[..., :half_width]
    trailing = values[..., half_width:]
    return jnp.concatenate(
        [leading * cosine - trailing * sine_table, trailing * cosine + leading * sine_table],
        axis=-1,
    )


def attend(full_query, keys, allowed, w_value):
    rows_here, head_count = (full_query.shape[0], full_query.shape[1])
    group_size = math.gcd(head_count, 4)
    groups = head_count // group_size
    grouped = full_query.reshape(rows_here, groups, group_size, KVR + ROPE).transpose(1, 0, 2, 3)
    value_blocks = w_value.reshape(KVR, groups, group_size, VD).transpose(1, 0, 2, 3)
    latent_values = keys[:, :KVR]
    scale = 1.0 / math.sqrt(NOPE + ROPE)

    def one_group(operands):
        chosen, w_group = operands
        scores = jnp.einsum("tgc,sc->tgs", chosen, keys, preferred_element_type=jnp.float32) * scale
        scores = jnp.where(allowed[:, None, :], scores, -1e30)
        row_max = jnp.max(scores, axis=-1, keepdims=True)
        lifted = jnp.exp(scores - row_max)
        weights = (lifted / jnp.sum(lifted, axis=-1, keepdims=True)).astype(jnp.bfloat16)
        context = jnp.einsum(
            "tgs,sc->tgc", weights, latent_values, preferred_element_type=jnp.float32
        ).astype(jnp.bfloat16)
        return jnp.einsum(
            "tgc,cgv->tgv", context, w_group, preferred_element_type=jnp.float32
        ).astype(jnp.bfloat16)

    outputs = lax.map(one_group, (grouped, value_blocks))
    return outputs.transpose(1, 0, 2, 3).reshape(rows_here, head_count * VD)


def local(q_latent, kv_latent, kv_gain, w_q_b, w_kv_b, w_o, prompt_len, response_mask):
    rows_here = q_latent.shape[0]
    offset = lax.axis_index("dp") * rows_here
    local_positions = offset + jnp.arange(rows_here, dtype=jnp.int32)
    cosine, sine_table = tables(local_positions)
    latent = kv_latent[:, :KVR].astype(jnp.float32)
    normed = (
        latent * lax.rsqrt(jnp.mean(latent * latent, axis=-1, keepdims=True) + epsilon) * kv_gain
    )
    key_rope = rotate(kv_latent[:, KVR:].astype(jnp.float32), cosine, sine_table)
    local_keys = jnp.concatenate([normed, key_rope], axis=1).astype(jnp.bfloat16)
    keys = lax.all_gather(local_keys, "dp", axis=0, tiled=True)
    head_count = w_q_b.shape[1] // (NOPE + ROPE)
    queries = jnp.dot(q_latent, w_q_b, preferred_element_type=jnp.float32).astype(jnp.bfloat16)
    queries = queries.reshape(rows_here, head_count, NOPE + ROPE)
    query_rope = rotate(
        queries[:, :, NOPE:].astype(jnp.float32), cosine[:, None, :], sine_table[:, None, :]
    ).astype(jnp.bfloat16)
    w_heads = w_kv_b.reshape(KVR, head_count, NOPE + VD)
    absorbed = jnp.einsum(
        "thn,khn->thk",
        queries[:, :, :NOPE],
        w_heads[:, :, :NOPE],
        preferred_element_type=jnp.float32,
    ).astype(jnp.bfloat16)
    full_query = jnp.concatenate([absorbed, query_rope], axis=-1)
    key_positions = jnp.arange(keys.shape[0], dtype=jnp.int32)
    usable = (key_positions < prompt_len[0]) | (response_mask == 1)
    allowed = (key_positions[None, :] <= local_positions[:, None]) & usable[None, :]
    attended = attend(full_query, keys, allowed, w_heads[:, :, NOPE:])
    spread = jnp.dot(
        lax.all_gather(attended, "dp", axis=0, tiled=True), w_o, preferred_element_type=jnp.float32
    )
    partial_value = lax.all_to_all(spread, "dp", split_axis=0, concat_axis=1, tiled=True)
    return lax.psum_scatter(partial_value, "head", scatter_dimension=1, tiled=True).astype(
        jnp.bfloat16
    )


def solution(mesh):
    return jax.shard_map(
        local,
        mesh=mesh,
        in_specs=(
            P("dp", None),
            P("dp", None),
            P(),
            P(None, "head"),
            P(None, "head"),
            P("head", "dp"),
            P(),
            P(),
        ),
        out_specs=P("dp", "head"),
        check_vma=False,
    )
```

profile of v0, /device:TPU:25, one launch (start us, length us, event | category | flops | bytes accessed | tf_op | source)
XLA Modules:
  0.0 299.7 jit_solution(449969691747833988)
XLA Ops:
  8.3 1.1 fusion.45
  10.3 6.5 %copy.17 = bf16[512,4096]{0,1:T(8,128)(2,1)} copy(bf16[512,4096]{1,0:T(8,128)(2,1)} %param.14) | data formatting | bytes 8388608 | tf_op args[4]
  16.8 3.1 %slice.44 = bf16[512,16,128]{0,2,1:T(8,128)(2,1)} slice(bf16[512,16,256]{0,2,1:T(8,128)(2,1)} %bitcast.67), slice={[0:512], [0:16], [128:256]} | slice | bytes 4194304 | tf_op jit(solution)/shard_map/slice | solution.py:90
  19.9 5.1 %convolution_convert_fusion.1 = bf16[128,3072]{1,0:T(8,128)(2,1)S(1)} fusion(bf16[128,1536]{1,0:T(8,128)(2,1)S(1)} %copy-done, bf16[1536,3072]{1,0:T(8,128)(2,1)} %param.13), kind=kOutput, calls=%fused_computation.28 | convolution fusion | flops 1208352768 | bytes 10616832 | tf_op jit(solution)/shard_map/dot_general | solution.py:74
  26.5 2.4 convert_bitcast_fusion
  29.3 2.6 copy.24
  32.6 15.6 %all-gather.3.cloned.1.call-done = bf16[1024,576]{0,1:T(8,128)(2,1)} async-done(((bf16[128,576]{0,1:T(8,128)(2,1)}), bf16[1024,576]{0,1:T(8,128)(2,1)}) %all-gather.3.cloned.1.call-update) | async-done | bytes 1179664 | tf_op jit(solution)/shard_map/all_gather | solution.py:72
  48.2 1.2 slice-done
  49.4 1.3 copy.30
  50.7 28.2 %while.11 = (s32[]{:T(128)}, bf16[4,128,4,128]{1,3,2,0:T(8,128)(2,1)S(1)}, bf16[4,512,4,128]{1,3,2,0:T(8,128)(2,1)}, bf16[4,128,4,576]{1,3,2,0:T(8,128)(2,1)}, b...) while((s32[]{:T(128)}, ...), condition=%wide.region_4.5_spmd.clone, body=%wide.region_1.4_spmd.clone.sunk | while | flops 1211696128 | bytes 7936617 | solution.py:57
  50.9 3.9 %fusion.70 = (f32[128,4]{0,1:T(4,128)S(1)}, f32[128,4,1024]{2,0,1:T(8,128)}) fusion(pred[128,1024]{1,0:T(8,128)(4,1)S(1)} %fusion.69, bf16[1024,576]{0,1:T(8,128)(2,1)S(1)} %get-tuple-element.162, bf16[4,128,4,576]{1,3,2,0:T(8,128)(2,1)} %get-tuple-element.161, s32[]{:T(128)S(6)} %copy.35), kind=kOutput, calls=%fused_computation.53.clone.1 | convolution fusion | flops 606077952 | bytes 3999748 | tf_op jit(solution)/shard_map/while/body/eval_jaxpr/sub | solution.py:48
  54.7 3.0 %fusion.71 = bf16[4,128,4,128]{1,3,2,0:T(8,128)(2,1)S(1)} fusion(bf16[4,128,4,128]{1,3,2,0:T(8,128)(2,1)S(1)} %get-tuple-element.150, s32[]{:T(128)S(6)} %copy.35, bf16[1024,512]{1,0:T(8,128)(2,1)} %get-tuple-element.163, f32[128,4,1024]{2,0,1:T(8,128)} %get-tuple-element.138, f32[128,4]{0,1:T(4,128)S(1)} %get-tuple-element.139, ...), kind=kOutput, calls=%fused_computation.12.clone.1 | convolution fusion | flops 605356032 | bytes 3804160 | tf_op jit(solution)/shard_map/while/body/eval_jaxpr/tgc,cgv->tgv/dot_general | solution.py:53
  57.9 3.9 %fusion.70 = (f32[128,4]{0,1:T(4,128)S(1)}, f32[128,4,1024]{2,0,1:T(8,128)}) fusion(pred[128,1024]{1,0:T(8,128)(4,1)S(1)} %fusion.69, bf16[1024,576]{0,1:T(8,128)(2,1)S(1)} %get-tuple-element.162, bf16[4,128,4,576]{1,3,2,0:T(8,128)(2,1)} %get-tuple-element.161, s32[]{:T(128)S(6)} %copy.35), kind=kOutput, calls=%fused_computation.53.clone.1 | convolution fusion | flops 606077952 | bytes 3999748 | tf_op jit(solution)/shard_map/while/body/eval_jaxpr/sub | solution.py:48
  61.8 3.0 %fusion.71 = bf16[4,128,4,128]{1,3,2,0:T(8,128)(2,1)S(1)} fusion(bf16[4,128,4,128]{1,3,2,0:T(8,128)(2,1)S(1)} %get-tuple-element.150, s32[]{:T(128)S(6)} %copy.35, bf16[1024,512]{1,0:T(8,128)(2,1)} %get-tuple-element.163, f32[128,4,1024]{2,0,1:T(8,128)} %get-tuple-element.138, f32[128,4]{0,1:T(4,128)S(1)} %get-tuple-element.139, ...), kind=kOutput, calls=%fused_computation.12.clone.1 | convolution fusion | flops 605356032 | bytes 3804160 | tf_op jit(solution)/shard_map/while/body/eval_jaxpr/tgc,cgv->tgv/dot_general | solution.py:53
  65.0 3.9 %fusion.70 = (f32[128,4]{0,1:T(4,128)S(1)}, f32[128,4,1024]{2,0,1:T(8,128)}) fusion(pred[128,1024]{1,0:T(8,128)(4,1)S(1)} %fusion.69, bf16[1024,576]{0,1:T(8,128)(2,1)S(1)} %get-tuple-element.162, bf16[4,128,4,576]{1,3,2,0:T(8,128)(2,1)} %get-tuple-element.161, s32[]{:T(128)S(6)} %copy.35), kind=kOutput, calls=%fused_computation.53.clone.1 | convolution fusion | flops 606077952 | bytes 3999748 | tf_op jit(solution)/shard_map/while/body/eval_jaxpr/sub | solution.py:48
  68.9 3.0 %fusion.71 = bf16[4,128,4,128]{1,3,2,0:T(8,128)(2,1)S(1)} fusion(bf16[4,128,4,128]{1,3,2,0:T(8,128)(2,1)S(1)} %get-tuple-element.150, s32[]{:T(128)S(6)} %copy.35, bf16[1024,512]{1,0:T(8,128)(2,1)} %get-tuple-element.163, f32[128,4,1024]{2,0,1:T(8,128)} %get-tuple-element.138, f32[128,4]{0,1:T(4,128)S(1)} %get-tuple-element.139, ...), kind=kOutput, calls=%fused_computation.12.clone.1 | convolution fusion | flops 605356032 | bytes 3804160 | tf_op jit(solution)/shard_map/while/body/eval_jaxpr/tgc,cgv->tgv/dot_general | solution.py:53
  72.1 3.9 %fusion.70 = (f32[128,4]{0,1:T(4,128)S(1)}, f32[128,4,1024]{2,0,1:T(8,128)}) fusion(pred[128,1024]{1,0:T(8,128)(4,1)S(1)} %fusion.69, bf16[1024,576]{0,1:T(8,128)(2,1)S(1)} %get-tuple-element.162, bf16[4,128,4,576]{1,3,2,0:T(8,128)(2,1)} %get-tuple-element.161, s32[]{:T(128)S(6)} %copy.35), kind=kOutput, calls=%fused_computation.53.clone.1 | convolution fusion | flops 606077952 | bytes 3999748 | tf_op jit(solution)/shard_map/while/body/eval_jaxpr/sub | solution.py:48
  75.9 3.0 %fusion.71 = bf16[4,128,4,128]{1,3,2,0:T(8,128)(2,1)S(1)} fusion(bf16[4,128,4,128]{1,3,2,0:T(8,128)(2,1)S(1)} %get-tuple-element.150, s32[]{:T(128)S(6)} %copy.35, bf16[1024,512]{1,0:T(8,128)(2,1)} %get-tuple-element.163, f32[128,4,1024]{2,0,1:T(8,128)} %get-tuple-element.138, f32[128,4]{0,1:T(4,128)S(1)} %get-tuple-element.139, ...), kind=kOutput, calls=%fused_computation.12.clone.1 | convolution fusion | flops 605356032 | bytes 3804160 | tf_op jit(solution)/shard_map/while/body/eval_jaxpr/tgc,cgv->tgv/dot_general | solution.py:53
  79.8 75.2 %all-gather.5.cloned.1.call-done = bf16[1024,2048]{0,1:T(8,128)(2,1)} async-done(((bf16[128,2048]{0,1:T(8,128)(2,1)}), bf16[1024,2048]{0,1:T(8,128)(2,1)}) %all-gather.5.cloned.1.call-update) | async-done | bytes 4194320 | tf_op jit(solution)/shard_map/all_gather | solution.py:92
  155.1 7.4 %fusion.53 = f32[1024,896]{1,0:T(8,128)S(1)} fusion(bf16[1024,2048]{0,1:T(8,128)(2,1)} %all-gather.5.cloned.1.call-done, bf16[2048,896]{1,0:T(8,128)(2,1)} %param.15), kind=kOutput, calls=%fused_computation.54 | convolution fusion | flops 3758096384 | bytes 11534336 | tf_op jit(solution)/shard_map/dot_general | solution.py:91
  162.5 83.8 %all_to_all.19 = f32[8,128,896]{2,1,0:T(8,128)S(1)} all-to-all(f32[8,128,896]{2,1,0:T(8,128)S(1)} %bitcast.72), channel_id=1, replica_groups=mesh['dp'=8,'head'=4] {'dp'}, dimensions={0} | all-to-all | bytes 7340032 | tf_op jit(solution)/shard_map/all_to_all | solution.py:94
  246.3 2.2 copy.31
  248.5 42.7 %reduce-scatter.2.cloned.1.call-done = f32[128,1792]{1,0:T(8,128)} async-done(((f32[128,7168]{1,0:T(8,128)}), f32[128,1792]{1,0:T(8,128)}) %reduce-scatter.2.cloned.1.call-update) | async-done | bytes 917520 | tf_op jit(solution)/shard_map/reduce_scatter | solution.py:95
  291.2 2.0 convert_element_type.49
  (37 shorter events, 6.1 us)
Async XLA Ops:
  6.5 13.3 %copy-start = (bf16[128,1536]{1,0:T(8,128)(2,1)S(1)}, bf16[128,1536]{1,0:T(8,128)(2,1)}, u32[]{:S(2)}) copy-start(bf16[128,1536]{1,0:T(8,128)(2,1)} %param.10) | copy-start | bytes 1179652
  6.5 41.6 %all-gather.3.cloned.1.call-start = ((), (), s32[]{:S(2)}) async-start(), calls=%async_computation.2 | async-start | bytes 1327104 | tf_op jit(solution)/shard_map/all_gather | solution.py:72
  10.2 144.8 %all-gather.5.cloned.1.call-start = ((), (), s32[]{:S(2)}) async-start(), calls=%async_computation.3 | async-start | bytes 4718592 | tf_op jit(solution)/shard_map/all_gather | solution.py:92
  29.3 3.2 %copy-start.3 = (s32[1024]{0:T(1024)S(1)}, s32[1024]{0:T(1024)}, u32[]{:S(2)}) copy-start(s32[1024]{0:T(1024)} %param.17) | copy-start | bytes 12292
  48.2 1.2 slice-start
  48.2 2.5 copy-start.1
  79.0 0.8 copy-start.2
  79.8 211.4 %reduce-scatter.2.cloned.1.call-start = ((), (), s32[]{:S(2)}) async-start(), calls=%async_computation.4 | async-start | bytes 4587520 | tf_op jit(solution)/shard_map/reduce_scatter | solution.py:95
Sparse Core Ops, SparseCore 0:
  10.4 37.7 all-gather.2
  79.9 75.1 all-gather.4
  248.6 42.5 reduce-scatter.1
where the time goes:
time: 302 us; the launch traced here: 300 us
  waiting for transfers between devices  134 us (44%)
  blocking collectives  83.8 us (28%)
  matrix products  42.4 us (14%)
  local copies, waits for them, and re-layouts  18.5 us (6%)
  between operations  13.9 us (5%)
  other arithmetic  7.33 us (2%)
    all_to_all x1, blocking collectives, local(): lax.all_to_all(spread, 'dp', split_axis=0, concat_axis=1, tiled=True)  83.8 us
    all_gather x1, waiting for transfers between devices, local(): lax.all_gather(attended, 'dp', axis=0, tiled=True)  75.2 us
    reduce_scatter x1, waiting for transfers between devices, local(): lax.psum_scatter(partial_value, 'head', scatter_dimension=1, tiled=True)  42.7 us
    all_gather x1, waiting for transfers between devices, local(): keys = lax.all_gather(local_keys, 'dp', axis=0, tiled=True)  15.6 us
    sub x4, matrix products, one_group(): lifted = jnp.exp(scores - row_max)  15.5 us
    dot_general x4, matrix products, one_group(): jnp.einsum('tgc,cgv->tgv', context, w_group, preferred_element_type=jnp.f...  12.1 us
    unnamed x11, local copies, waits for them, and re-layouts  8.87 us
    dot_general x1, matrix products, local(): jnp.dot(lax.all_gather(attended, 'dp', axis=0, tiled=True), w_o, preferre...  7.38 us
  transfers between devices with their start and end apart: 3, of which 3 were waited for; matrix products, arithmetic and copies ran while one was open for 7% of the time, Pallas kernels for 0%

commit v1 on v0

--- a/solution.py
+++ b/solution.py
@@ -1,8 +1,11 @@
+import functools
 import math
 
 import jax
 import jax.numpy as jnp
 from jax import lax
+from jax.experimental import pallas as pl
+from jax.experimental.pallas import tpu as pltpu
 from jax.sharding import PartitionSpec as P
 
 KVR = 512
@@ -97,9 +100,350 @@
     )
 
 
+MESH = pl.DeviceIdType.MESH
+LOG2E = 1.4426950408889634
+QB = 256
+
+
+def gather_kernel(n, x_ref, out_ref, own_sem, send_sem, recv_sem, psend_sem, precv_sem):
+    me = lax.axis_index("dp")
+    g = lax.axis_index("head")
+    half = n // 2
+    rows = x_ref.shape[0]
+    part = rows // 2
+    core = lax.rem(g, 2)
+    mate = g + 1 - 2 * core
+    start = core * part
+
+    def place(j):
+        return lax.rem(j, 2) * (n - 1 - j // 2) + (1 - lax.rem(j, 2)) * (j // 2)
+
+    def owner(p):
+        upper = p // half
+        return (1 - upper) * (2 * p) + upper * (2 * (n - 1 - p) + 1)
+
+    here = place(me)
+    right = owner(lax.rem(here + 1, n))
+    left = owner(lax.rem(here + n - 1, n))
+
+    barrier = pltpu.get_barrier_semaphore()
+    pl.semaphore_signal(barrier, inc=1, device_id=(left, g), device_id_type=MESH)
+    pl.semaphore_signal(barrier, inc=1, device_id=(right, g), device_id_type=MESH)
+    pl.semaphore_signal(barrier, inc=1, device_id=(me, mate), device_id_type=MESH)
+    pl.semaphore_wait(barrier, 3)
+
+    own = pltpu.make_async_copy(x_ref, out_ref.at[me], own_sem)
+    own.start()
+
+    def span(step, way):
+        if step < half - 1:
+            return start, part
+        return start + way * (part // 2), part // 2
+
+    def ring(step, way, block, target):
+        first, count = span(step, way)
+        first = pl.multiple_of(first, count)
+        if step == 0:
+            source = x_ref.at[pl.ds(first, count)]
+        else:
+            source = out_ref.at[block, pl.ds(first, count)]
+        return pltpu.make_async_remote_copy(
+            src_ref=source,
+            dst_ref=out_ref.at[block, pl.ds(first, count)],
+            send_sem=send_sem.at[way, step],
+            recv_sem=recv_sem.at[way, step],
+            device_id=(target, g),
+            device_id_type=MESH,
+        )
+
+    def share(step, way, block):
+        first, count = span(step, way)
+        first = pl.multiple_of(first, count)
+        return pltpu.make_async_remote_copy(
+            src_ref=out_ref.at[block, pl.ds(first, count)],
+            dst_ref=out_ref.at[block, pl.ds(first, count)],
+            send_sem=psend_sem.at[way, step],
+            recv_sem=precv_sem.at[way, step],
+            device_id=(me, mate),
+            device_id_type=MESH,
+        )
+
+    rings, shares = [], []
+    for step in range(half):
+        right_copy = ring(step, 0, owner(lax.rem(here + n - step, n)), right)
+        left_copy = ring(step, 1, owner(lax.rem(here + step, n)), left)
+        right_copy.start()
+        left_copy.start()
+        rings += [right_copy, left_copy]
+        right_copy.wait_recv()
+        copy = share(step, 0, owner(lax.rem(here + n - step - 1, n)))
+        copy.start()
+        shares.append(copy)
+        left_copy.wait_recv()
+        copy = share(step, 1, owner(lax.rem(here + step + 1, n)))
+        copy.start()
+        shares.append(copy)
+    own.wait()
+    for copy in rings:
+        copy.wait_send()
+    for copy in shares:
+        copy.wait()
+
+
+def compute_kernel(
+    x_hbm, wq_hbm, wkv_hbm, wo_hbm, gain_ref, cosk_ref, sink_ref, cq_ref, sa_ref, sb_ref, bias_ref,
+    out_ref,
+    x, wq, wkv, wo, keys, kslab, vbuf, att, mask, sems,
+):
+    tokens = x.shape[0]
+    qr = wq.shape[0]
+    pairs = wkv.shape[1] // (2 * (NOPE + VD))
+    copies = [
+        pltpu.make_async_copy(x_hbm, x, sems.at[0]),
+        pltpu.make_async_copy(wkv_hbm, wkv, sems.at[1]),
+        pltpu.make_async_copy(wq_hbm, wq, sems.at[2]),
+        pltpu.make_async_copy(wo_hbm, wo, sems.at[3]),
+    ]
+    for copy in copies:
+        copy.start()
+    copies[0].wait()
+    scale = LOG2E / math.sqrt(NOPE + ROPE)
+
+    latent = x[:, qr : qr + KVR].astype(jnp.float32)
+    mean = jnp.mean(latent * latent, axis=-1, keepdims=True)
+    keys[...] = (latent * lax.rsqrt(mean + epsilon) * gain_ref[...]).astype(jnp.bfloat16)
+    rope = x[:, qr + KVR :].astype(jnp.float32)
+    half = ROPE // 2
+    turned = jnp.concatenate([-rope[:, half:], rope[:, :half]], axis=1)
+    key_rope = (rope * cosk_ref[...] + turned * sink_ref[...]).astype(jnp.bfloat16)
+    blank = jnp.zeros((tokens, NOPE - ROPE), jnp.bfloat16)
+    even_tail = jnp.concatenate([key_rope, blank], axis=1)
+    for p in range(pairs):
+        kslab[p, :, 128:256] = even_tail
+    copies[1].wait()
+
+    @pl.loop(0, pairs)
+    def _(p):
+        width = 2 * (NOPE + VD)
+        w = wkv[:, pl.ds(pl.multiple_of(p * width, width), width)]
+        for r in range(tokens // QB):
+            rows = slice(r * QB, (r + 1) * QB)
+            both = jnp.dot(keys[rows, :], w, preferred_element_type=jnp.float32).astype(jnp.bfloat16)
+            kslab[p, rows, 0:128] = both[:, 0:128]
+            vbuf[p, rows, 0:128] = both[:, 128:256]
+            vbuf[p, rows, 128:256] = both[:, 384:512]
+            odd = both[:, 256:384]
+            kslab[p, rows, 256:384] = jnp.concatenate([blank[rows], odd[:, :64]], axis=1)
+            kslab[p, rows, 384:512] = jnp.concatenate([odd[:, 64:], kslab[p, rows, 128:192]], axis=1)
+
+    copies[2].wait()
+    for r in range(tokens // QB):
+        rows = slice(r * QB, (r + 1) * QB)
+        end = (r + 1) * QB
+        row_ids = r * QB + lax.broadcasted_iota(jnp.int32, (QB, end), 0)
+        col_ids = lax.broadcasted_iota(jnp.int32, (QB, end), 1)
+        mask[:, :end] = jnp.where(col_ids <= row_ids, bias_ref[:, :end], -1e30)
+
+        @pl.loop(0, pairs)
+        def _(p):
+            w = wq[:, pl.ds(pl.multiple_of(p * 384, 384), 384)]
+            q = jnp.dot(x[rows, :qr], w, preferred_element_type=jnp.float32).astype(jnp.bfloat16)
+            v = q[:, 128:384].astype(jnp.float32)
+            v = (
+                v * cq_ref[rows, :]
+                + pltpu.roll(v, 256 - half, 1) * sa_ref[rows, :]
+                + pltpu.roll(v, half, 1) * sb_ref[rows, :]
+            ).astype(jnp.bfloat16)
+            slabs = (jnp.concatenate([q[:, :128], v[:, :128]], axis=1), v)
+            for h in range(2):
+                s = lax.dot_general(
+                    slabs[h], kslab[p, :end, 256 * h : 256 * h + 256],
+                    (((1,), (1,)), ((), ())), preferred_element_type=jnp.float32,
+                )
+                s = s * scale + mask[:, :end]
+                top = jnp.max(s, axis=-1, keepdims=True)
+                e = jnp.exp2(s - top)
+                total = jnp.sum(e, axis=-1, keepdims=True)
+                o = jnp.dot(
+                    e.astype(jnp.bfloat16), vbuf[p, :end, 128 * h : 128 * h + 128],
+                    preferred_element_type=jnp.float32,
+                )
+                at = pl.ds(pl.multiple_of(p * 256 + 128 * h, 128), 128)
+                att[:, at] = (o / total).astype(jnp.bfloat16)
+
+        if r == 0:
+            copies[3].wait()
+        out_ref[rows, :] = jnp.dot(att[...], wo[...], preferred_element_type=jnp.float32).astype(jnp.bfloat16)
+
+
+def reduce_kernel(n, heads, part_ref, out_ref, from_mate, summed, arrived, msend, mrecv, send_sem, recv_sem):
+    me = lax.axis_index("dp")
+    g = lax.axis_index("head")
+    core = lax.rem(g, 2)
+    mate = g + 1 - 2 * core
+    side = g // 2
+    sides = heads // 2
+    per = n // heads
+    target = me // per
+    slot = lax.rem(me, per) * sides + side
+    cols = part_ref.shape[2]
+
+    first = []
+    for k in range(n // 2):
+        copy = pltpu.make_async_remote_copy(
+            src_ref=part_ref.at[2 * k + 1 - core],
+            dst_ref=from_mate.at[k],
+            send_sem=msend.at[k],
+            recv_sem=mrecv.at[k],
+            device_id=(me, mate),
+            device_id_type=MESH,
+        )
+        copy.start()
+        first.append(copy)
+
+    def second(k):
+        return pltpu.make_async_remote_copy(
+            src_ref=summed.at[k],
+            dst_ref=arrived.at[slot],
+            send_sem=send_sem.at[k],
+            recv_sem=recv_sem.at[slot],
+            device_id=(2 * k + core, target),
+            device_id_type=MESH,
+        )
+
+    for k in range(n // 2):
+        first[k].wait_recv()
+        summed[k] = (
+            part_ref[2 * k + core].astype(jnp.float32) + from_mate[k].astype(jnp.float32)
+        ).astype(jnp.bfloat16)
+        mine = (2 * k + core == me) & (target == g)
+
+        @pl.when(mine)
+        def _():
+            arrived[slot] = summed[k]
+
+        @pl.when(jnp.logical_not(mine))
+        def _():
+            second(k).start()
+
+    for a in range(per):
+        for b in range(sides):
+            source = g * per + a
+            mine = (source == me) & (lax.rem(me, 2) == core) & (b == side)
+
+            @pl.when(jnp.logical_not(mine))
+            def _():
+                pltpu.make_async_remote_copy(
+                    src_ref=summed.at[0],
+                    dst_ref=arrived.at[a * sides + b],
+                    send_sem=send_sem.at[0],
+                    recv_sem=recv_sem.at[a * sides + b],
+                    device_id=(source, g),
+                    device_id_type=MESH,
+                ).wait_recv()
+
+        total = arrived[a * sides].astype(jnp.float32)
+        for b in range(1, sides):
+            total = total + arrived[a * sides + b].astype(jnp.float32)
+        out_ref[:, a * cols : (a + 1) * cols] = total.astype(jnp.bfloat16)
+
+    for k in range(n // 2):
+        mine = (2 * k + core == me) & (target == g)
+
+        @pl.when(jnp.logical_not(mine))
+        def _():
+            second(k).wait_send()
+
+        first[k].wait_send()
+
+
+ANY = pl.BlockSpec(memory_space=pl.ANY)
+VMEM = pl.BlockSpec(memory_space=pltpu.VMEM)
+
+
+def fused(n, heads, q_latent, kv_latent, kv_gain, w_q_b, w_kv_b, w_o, prompt_len, response_mask):
+    rows, qr = q_latent.shape
+    tokens = rows * n
+    width = qr + KVR + ROPE
+    cols = w_o.shape[1]
+    pairs = w_kv_b.shape[1] // (2 * (NOPE + VD))
+    x = jnp.concatenate([q_latent, kv_latent], axis=1)
+    steps = n // 2
+    gathered = pl.pallas_call(
+        functools.partial(gather_kernel, n),
+        out_shape=jax.ShapeDtypeStruct((n, rows, width), jnp.bfloat16),
+        in_specs=[VMEM],
+        out_specs=ANY,
+        scratch_shapes=[pltpu.SemaphoreType.DMA] + [pltpu.SemaphoreType.DMA((2, steps))] * 4,
+        compiler_params=pltpu.CompilerParams(collective_id=0, has_side_effects=True),
+        name="gather_rows",
+    )(x).reshape(tokens, width)
+
+    positions = jnp.arange(tokens, dtype=jnp.int32)
+    cosine, sine_table = tables(positions)
+    one = jnp.ones((tokens, NOPE), jnp.float32)
+    none = jnp.zeros((tokens, NOPE), jnp.float32)
+    zero = jnp.zeros_like(sine_table)
+    cosk = jnp.concatenate([cosine, cosine], axis=1)
+    sink = jnp.concatenate([sine_table, sine_table], axis=1)
+    cq = jnp.concatenate([cosk, one, cosk], axis=1)
+    sa = jnp.concatenate([-sine_table, zero, none, -sine_table, zero], axis=1)
+    sb = jnp.concatenate([zero, sine_table, none, zero, sine_table], axis=1)
+    usable = (positions < prompt_len[0]) | (response_mask == 1)
+    bias = jnp.where(usable, 0.0, -1e30).astype(jnp.float32)[None, :]
+    bf = jnp.bfloat16
+    partial_sum = pl.pallas_call(
+        compute_kernel,
+        out_shape=jax.ShapeDtypeStruct((tokens, cols), bf),
+        in_specs=[ANY] * 4 + [VMEM] * 7,
+        out_specs=VMEM,
+        scratch_shapes=[
+            pltpu.VMEM((tokens, width), bf),
+            pltpu.VMEM(w_q_b.shape, bf),
+            pltpu.VMEM(w_kv_b.shape, bf),
+            pltpu.VMEM(w_o.shape, bf),
+            pltpu.VMEM((tokens, KVR), bf),
+            pltpu.VMEM((pairs, tokens, 512), bf),
+            pltpu.VMEM((pairs, tokens, 2 * VD), bf),
+            pltpu.VMEM((QB, 2 * pairs * VD), bf),
+            pltpu.VMEM((QB, tokens), jnp.float32),
+            pltpu.SemaphoreType.DMA((4,)),
+        ],
+        compiler_params=pltpu.CompilerParams(vmem_limit_bytes=60 * 1024 * 1024),
+        name="attend_project",
+    )(gathered, w_q_b, w_kv_b, w_o, kv_gain[None, :], cosk, sink, cq, sa, sb, bias)
+
+    half = n // 2
+    slots = (n // heads) * (heads // 2)
+    return pl.pallas_call(
+        functools.partial(reduce_kernel, n, heads),
+        out_shape=jax.ShapeDtypeStruct((rows, cols * (n // heads)), bf),
+        in_specs=[VMEM],
+        out_specs=VMEM,
+        scratch_shapes=[
+            pltpu.VMEM((half, rows, cols), bf),
+            pltpu.VMEM((half, rows, cols), bf),
+            pltpu.VMEM((slots, rows, cols), bf),
+            pltpu.SemaphoreType.DMA((half,)),
+            pltpu.SemaphoreType.DMA((half,)),
+            pltpu.SemaphoreType.DMA((half,)),
+            pltpu.SemaphoreType.DMA((slots,)),
+        ],
+        compiler_params=pltpu.CompilerParams(has_side_effects=True),
+        name="reduce_rows",
+    )(partial_sum.reshape(n, rows, cols))
+
+
 def solution(mesh):
+    n, heads = mesh.shape["dp"], mesh.shape["head"]
+
+    def step(*arrays):
+        rows, cols = arrays[0].shape[0], arrays[5].shape[1]
+        fits = rows * n <= 1024 and cols % 128 == 0 and n % heads == 0 and heads % 2 == 0
+        return fused(n, heads, *arrays) if fits else local(*arrays)
+
     return jax.shard_map(
-        local,
+        step,
         mesh=mesh,
         in_specs=(
             P("dp", None),

time: 302 us -> 144 us (0.48)
  waiting for transfers between devices: 134 us -> 0 us
  Pallas kernels: 0 us -> 128 us
  blocking collectives: 83.8 us -> 0 us
  matrix products: 42.4 us -> 0 us
  between operations: 13.9 us -> 0.71 us
  local copies, waits for them, and re-layouts: 18.5 us -> 8.29 us
    pallas_call x0 -> x3, Pallas kernels: none -> 128 us  [the longest x1 64.1 us: fused(): pl.pallas_call(compute_kernel, out_shape=jax.ShapeDtypeStruct((tokens, co...]
    all_gather x2 -> x0, waiting for transfers between devices: 90.8 us -> none  [the longest x1 75.2 us: local(): lax.all_gather(attended, 'dp', axis=0, tiled=True)]
    all_to_all x1 -> x0, blocking collectives: 83.8 us -> none  [local(): lax.all_to_all(spread, 'dp', split_axis=0, concat_axis=1, tiled=True)]
    reduce_scatter x1 -> x0, waiting for transfers between devices: 42.7 us -> none  [local(): lax.psum_scatter(partial_value, 'head', scatter_dimension=1, tiled=True)]
    dot_general x7 -> x0, matrix products: 26.9 us -> none  [the longest x4 12.1 us: one_group(): jnp.einsum('tgc,cgv->tgv', context, w_group, preferred_element_type=jnp.f...]
    sub x4 -> x0, matrix products: 15.5 us -> none  [one_group(): lifted = jnp.exp(scores - row_max)]
    unnamed x11 -> x2, local copies, waits for them, and re-layouts: 8.87 us -> 2.88 us
    concatenate x0 -> x3, local copies, waits for them, and re-layouts: none -> 5.31 us  [the longest x1 1.89 us: fused(): sa = jnp.concatenate([-sine_table, zero, none, -sine_table, zero], axis=1)]
  transfers between devices with their start and end apart: 3 -> 0, of which waited for: 3 -> 0; matrix products, arithmetic and copies ran while one was open for 7% -> 0% of each run, Pallas kernels for 0% -> 0%
where the time goes in v1:
time: 144 us
  Pallas kernels  128 us (89%)
  local copies, waits for them, and re-layouts  8.29 us (6%)
  other arithmetic  6.35 us (4%)
    pallas_call x1, Pallas kernels, fused(): pl.pallas_call(compute_kernel, out_shape=jax.ShapeDtypeStruct((tokens, co...  64.1 us
    pallas_call x1, Pallas kernels, fused(): pl.pallas_call(functools.partial(reduce_kernel, n, heads), out_shape=jax....  33.9 us
    pallas_call x1, Pallas kernels, fused(): pl.pallas_call(functools.partial(gather_kernel, n), out_shape=jax.ShapeDt...  30.5 us

profile of v1, /device:TPU:25, one launch (start us, length us, event | category | flops | bytes accessed | tf_op | source)
XLA Modules:
  0.0 143.8 jit_solution(7821261829950931634)
XLA Ops:
  0.7 1.3 fusion.2
  2.0 1.1 copy.9
  3.0 1.8 %pad_maximum_fusion.x_ref = bf16[128,2112]{1,0:T(8,128)(2,1)} fusion(bf16[128,576]{1,0:T(8,128)(2,1)S(1)} %copy.9, bf16[128,1536]{1,0:T(8,128)(2,1)} %param.8), kind=kLoop, calls=%fused_computation.2 | loop fusion | flops 1081344 | bytes 1081344 | tf_op jit(solution)/shard_map/concatenate | solution.py:370
  4.9 1.9 %fusion = (f32[1024,32]{1,0:T(8,128)S(1)}, f32[1024,32]{1,0:T(8,128)S(1)}, f32[1024,32]{1,0:T(8,128)S(1)}) fusion(f32[32]{0:T(128)S(1)} %multiply_power_fusion, f32[1024]{0:T(1024)S(1)} %iota_convert_fusion), kind=kLoop, calls=%fused_computation.5 | loop fusion | flops 65536 | bytes 397440 | tf_op jit(solution)/shard_map/neg | solution.py:390
  6.9 1.9 %concatenate.23.sa_ref = f32[1024,256]{1,0:T(8,128)} concatenate(f32[1024,32]{1,0:T(8,128)S(1)} %get-tuple-element.5, f32[1024,32]{1,0:T(8,128)S(1)} %broadcast_in_dim.27, f32[1024,128]{1,0:T(8,128)S(1)} %broadcast_in_dim.28, f32[1024,32]{1,0:T(8,128)S(1)} %get-tuple-element.5, f32[1024,32]{1,0:T(8,128)S(1)} %broadcast_in_dim.27), dimensions={1} | concatenate | bytes 2097152 | tf_op jit(solution)/shard_map/concatenate | solution.py:390
  8.7 1.7 %concatenate.24.sb_ref = f32[1024,256]{1,0:T(8,128)} concatenate(f32[1024,32]{1,0:T(8,128)S(1)} %broadcast_in_dim.27, f32[1024,32]{1,0:T(8,128)S(1)} %get-tuple-element.6, f32[1024,128]{1,0:T(8,128)S(1)} %broadcast_in_dim.28, f32[1024,32]{1,0:T(8,128)S(1)} %broadcast_in_dim.27, f32[1024,32]{1,0:T(8,128)S(1)} %get-tuple-element.6), dimensions={1} | concatenate | bytes 2097152 | tf_op jit(solution)/shard_map/concatenate | solution.py:391
  10.5 1.7 %concatenate.22.cq_ref = f32[1024,256]{1,0:T(8,128)} concatenate(f32[1024,32]{1,0:T(8,128)S(1)} %get-tuple-element.7, f32[1024,32]{1,0:T(8,128)S(1)} %get-tuple-element.7, f32[1024,128]{1,0:T(8,128)S(1)} %broadcast_in_dim.26, f32[1024,32]{1,0:T(8,128)S(1)} %get-tuple-element.7, f32[1024,32]{1,0:T(8,128)S(1)} %get-tuple-element.7), dimensions={1} | concatenate | bytes 2097152 | tf_op jit(solution)/shard_map/concatenate | solution.py:389
  12.2 1.3 pad_maximum_fusion.1
  13.5 30.5 %gather_rows.1 = bf16[8,128,2112]{2,1,0:T(8,128)(2,1)} custom-call(bf16[128,2112]{1,0:T(8,128)(2,1)} %pad_maximum_fusion.x_ref), custom_call_target="tpu_custom_call" | custom-call | tf_op jit(solution)/shard_map/gather_rows/pallas_call | solution.py:372
  44.0 64.1 %attend_project.1 = bf16[1024,896]{1,0:T(8,128)(2,1)} custom-call(bf16[1024,2112]{1,0:T(8,128)(2,1)} %bitcast.6, bf16[1536,3072]{1,0:T(8,128)(2,1)} %wq_hbm.1, bf16[512,4096]{1,0:T(8,128)(2,1)} %wkv_hbm.1, bf16[2048,896]{1,0:T(8,128)(2,1)} %wo_hbm.1, f32[1,512]{1,0:T(1,128)} %bitcast.9, f32[1024,64]{1,0:T(8,128)} %get-tuple-element.8.cosk_ref, ...), custom_call_target="tpu_custom_call" | custom-call | tf_op jit(solution)/shard_map/attend_project/pallas_call | solution.py:395
  108.1 33.9 %reduce_rows.1 = bf16[128,1792]{1,0:T(8,128)(2,1)} custom-call(bf16[8,128,896]{2,1,0:T(8,128)(2,1)} %bitcast.7), custom_call_target="tpu_custom_call" | custom-call | tf_op jit(solution)/shard_map/reduce_rows/pallas_call | solution.py:418
  142.0 1.8 %copy.12 = bf16[128,1792]{1,0:T(8,128)(2,1)} copy(bf16[128,1792]{1,0:T(8,128)(2,1)} %reduce_rows.1) | data formatting | bytes 917504
  (5 shorter events, 0.1 us)
